TPU v7x, 32 devices: a whole 2x2x4 slice. The times are simulated.
32 devices in a mesh: cfg: 2 (over y), space: 8 (over z, x), tm: 2 (over core).
Axes of the slice: x: 2, y: 2, z: 4, core: 2. Of those that a mesh axis runs over, the one named last changes fastest.
Arguments:
- eigvecs: bfloat16 [4, 2304, 3, 2, 128], P(('cfg', 'tm'), 'space'), parts along dimension 0, may hold values from -6 to 6
- perambulator: bfloat16 [4, 8, 4, 2, 128, 128], P(('cfg', 'tm'), None, None, None, 'space'), parts along dimension 0, may hold values from -1 to 4
- momenta: int32 [1, 3], replicated, may hold values from 1 to 3
- source_slots: int32 [2], replicated, may hold values from 0 to 7, as said below
- gamma_columns: int32 [12, 4], replicated, may hold values from 0 to 3, each once within a row
- gamma_phases: int32 [12, 4], replicated, may hold values from 0 to 3
Outputs:
- meson: float32 [4, 128, 1, 12, 2, 128], P(('cfg', 'tm'), 'space'), parts along dimension 0
There are 2 independent parts, one for each index of `cfg`. A program takes and returns all parts, laid end to end along the dimension named above; an argument that names none is the same for every part. Nothing has to cross between parts.
Inputs may be any that keep to these rules, and one draw needn't show every extreme that they name: `source_slots`: the two slots differ, and one of them is 7. `gamma_columns`: each row is a permutation of 0 to 3.
All inputs are finite; a program needn't handle non-finite values.
Results may differ from a plain program's by a relative error of at most 0.0049.
Values may be sent and summed in bfloat16 or wider, within the bound.
No kernel may reach another device: no remote copies, remote signals or barrier semaphores. Data moves between devices by JAX's collectives and lax.ppermute only.
A program may use at most 64 MiB of HBM per device.

v0:
```python
import math
import jax
import jax.numpy as jnp
from jax import lax
from jax.sharding import PartitionSpec as P

LY = 48
LZ = 48


def gamma_mixer(gamma_columns, gamma_phases):
    spin_ids = jnp.arange(4, dtype=jnp.int32)
    matches = (gamma_columns[:, :, None] == spin_ids[None, None, :]).astype(jnp.float32)
    real_sign = (gamma_phases == 0).astype(jnp.float32) - (gamma_phases == 2).astype(jnp.float32)
    imag_sign = (gamma_phases == 1).astype(jnp.float32) - (gamma_phases == 3).astype(jnp.float32)
    real_part = matches * real_sign[:, :, None]
    imag_part = matches * imag_sign[:, :, None]
    first_row = jnp.stack([real_part, -imag_part], axis=-1)
    second_row = jnp.stack([imag_part, real_part], axis=-1)
    return jnp.stack([first_row, second_row], axis=1)


def apply_gammas(blocks, gamma_mix, factor):
    return factor * jnp.einsum(
        "gostk,apstkb->apgob", gamma_mix, blocks, precision=lax.Precision.HIGHEST
    )


def phase_tables(momenta, site_ids, extent_x):
    coord_z = site_ids % LZ
    coord_y = site_ids // LZ % LY
    coord_x = site_ids // (LY * LZ)
    turns = (
        (momenta[:, 0:1] * coord_x[None, :] % extent_x).astype(jnp.float32) / extent_x
        + (momenta[:, 1:2] * coord_y[None, :] % LY).astype(jnp.float32) / LY
        + (momenta[:, 2:3] * coord_z[None, :] % LZ).astype(jnp.float32) / LZ
    )
    angles = 2.0 * math.pi * turns
    return (jnp.cos(angles), jnp.sin(angles))


def sink_vectors(vectors, picked):
    eig_count = picked.shape[-1]
    real_parts = []
    imag_parts = []
    for spin_index in range(4):
        real_tau = picked[spin_index, 0]
        imag_tau = picked[spin_index, 1]
        stacked = jnp.concatenate(
            [
                jnp.concatenate([real_tau, imag_tau], axis=1),
                jnp.concatenate([-imag_tau, real_tau], axis=1),
            ],
            axis=0,
        )
        product = jnp.dot(vectors, stacked, preferred_element_type=jnp.float32).astype(jnp.bfloat16)
        real_parts.append(product[:, :eig_count])
        imag_parts.append(product[:, eig_count:])
    return (jnp.stack(real_parts, axis=1), jnp.stack(imag_parts, axis=1))


def twisted(right_real, right_imag, cosine, sine):
    moment_count, site_count = cosine.shape
    shaped_real = right_real.astype(jnp.float32).reshape(1, site_count, 3, 4, -1)
    shaped_imag = right_imag.astype(jnp.float32).reshape(1, site_count, 3, 4, -1)
    cosine_wide = cosine.reshape(moment_count, site_count, 1, 1, 1)
    sine_wide = sine.reshape(moment_count, site_count, 1, 1, 1)
    wave_real = (cosine_wide * shaped_real - sine_wide * shaped_imag).astype(jnp.bfloat16)
    wave_imag = (sine_wide * shaped_real + cosine_wide * shaped_imag).astype(jnp.bfloat16)
    return (
        wave_real.reshape(moment_count, site_count * 3, 4, -1),
        wave_imag.reshape(moment_count, site_count * 3, 4, -1),
    )


def on_device(eigvecs, perambulator, momenta, source_slots, gamma_columns, gamma_phases):
    local_sites = eigvecs.shape[1]
    eig_count = eigvecs.shape[4]
    ranks = lax.axis_size("space")
    total_sites = local_sites * ranks
    extent_x = total_sites // (LY * LZ)
    factor = 1.0 / math.sqrt(12.0 * total_sites)
    site_ids = lax.axis_index("space") * local_sites + jnp.arange(local_sites, dtype=jnp.int32)
    cosine, sine = phase_tables(momenta, site_ids, extent_x)
    gamma_mix = gamma_mixer(gamma_columns, gamma_phases)
    gathered = lax.all_gather(perambulator, "space", axis=4, tiled=True)
    chosen = jnp.take(gathered, source_slots, axis=1)
    vectors = eigvecs[0].reshape(local_sites * 3, 2 * eig_count)
    left_real, left_imag = sink_vectors(vectors, chosen[0, 0])
    right_real, right_imag = sink_vectors(vectors, chosen[0, 1])
    wave_real, wave_imag = twisted(right_real, right_imag, cosine, sine)
    real_block = jnp.einsum(
        "rsa,rtb->astb", left_real, wave_real[0], preferred_element_type=jnp.float32
    ) + jnp.einsum("rsa,rtb->astb", left_imag, wave_imag[0], preferred_element_type=jnp.float32)
    imag_block = jnp.einsum(
        "rsa,rtb->astb", left_real, wave_imag[0], preferred_element_type=jnp.float32
    ) - jnp.einsum("rsa,rtb->astb", left_imag, wave_real[0], preferred_element_type=jnp.float32)
    per_momentum = [jnp.stack([real_block, imag_block], axis=3)]
    meson_rows = lax.psum_scatter(
        apply_gammas(jnp.stack(per_momentum, axis=1), gamma_mix, factor),
        "space",
        scatter_dimension=0,
        tiled=True,
    )
    results = [meson_rows]
    return jnp.stack(results, axis=0)


def solution(mesh):
    in_specs = (
        P(("cfg", "tm"), "space", None, None, None),
        P(("cfg", "tm"), None, None, None, "space", None),
        P(),
        P(),
        P(),
        P(),
    )
    out_specs = P(("cfg", "tm"), "space", None, None, None, None)
    return jax.shard_map(
        on_device, mesh=mesh, in_specs=in_specs, out_specs=out_specs, check_vma=False
    )
```

profile of v0, /device:TPU:0, one launch (start us, length us, event | category | flops | bytes accessed | tf_op | source)
XLA Modules:
  0.0 155.9 jit_solution(15535519684010389070)
XLA Ops:
  6.5 0.7 all-gather.2.cloned.1.call-update
  7.3 1.3 fusion.137
  8.6 1.3 fusion.109
  10.5 0.7 compare_select_fusion
  11.2 0.7 convert_subtract_fusion
  11.9 0.7 fusion.124
  12.6 0.7 compare_and_fusion
  13.3 49.2 %all-gather.2.cloned.1.call-done = bf16[1,8,4,2,128,128]{5,4,3,2,1,0:T(8,128)(2,1)} async-done(((bf16[1,8,4,2,16,128]{5,4,3,2,1,0:T(8,128)(2,1)}), bf16[1,8,4,2,128,128]{5,4,3,2,1,0:T(8,128)(2,1)}) %all-gather.2.cloned.1.call-update) | async-done | bytes 2097168 | tf_op jit(solution)/shard_map/all_gather | solution.py:86
  62.5 2.2 %gather_fusion = bf16[2,4,2,128,128]{4,3,2,1,0:T(8,128)(2,1)S(1)} fusion(bf16[8,4,2,128,128]{4,3,2,1,0:T(8,128)(2,1)} %bitcast.174, s32[1024]{0:T(1024)S(1)} %pad_clamp_fusion), kind=kCustom, calls=%fused_computation | custom fusion | bytes 1048584 | tf_op jit(solution)/shard_map/jit(_take)/gather | solution.py:87
  65.0 0.7 copy-done
  66.4 0.3 fusion.9
  66.7 0.3 fusion.10
  67.0 0.3 fusion.11
  67.6 0.3 fusion.13
  68.0 0.3 fusion.14
  68.3 1.1 fusion.26
  69.3 1.1 fusion.25
  70.4 1.1 fusion.6
  71.5 1.1 fusion.5
  72.5 1.5 maximum_bitcast_fusion
  74.0 2.7 %copy.13 = f32[128,4,4,2,128,1]{4,2,1,3,5,0:T(4,128)S(1)} copy(f32[128,4,4,2,128,1]{0,4,1,2,3,5:T(8,128)} %maximum_bitcast_fusion) | data formatting | bytes 4194304 | tf_op jit(solution)/shard_map/stack | solution.py:98
  76.7 3.8 %fusion = f32[128,1,12,2,128]{4,2,3,0,1:T(8,128)} fusion(f32[128,4,4,2,128,1]{4,2,1,3,5,0:T(4,128)S(1)} %copy.13, f32[12,1,4,4,2]{0,3,2,4,1:T(4,128)S(1)} %get-tuple-element.48, f32[12,1,4,4,2]{0,3,2,4,1:T(4,128)S(1)} %get-tuple-element.47), kind=kOutput, calls=%fused_computation.7 | convolution fusion | flops 151388928 | bytes 3673088 | tf_op jit(solution)/shard_map/gostk,apstkb->apgob/dot_general | solution.py:24
  80.6 66.7 %reduce-scatter.2.cloned.1.call-done = f32[16,1,12,2,128]{4,2,3,0,1:T(8,128)} async-done(((f32[128,1,12,2,128]{4,2,3,0,1:T(8,128)}), f32[16,1,12,2,128]{4,2,3,0,1:T(8,128)}) %reduce-scatter.2.cloned.1.call-update) | async-done | bytes 196624 | tf_op jit(solution)/shard_map/reduce_scatter | solution.py:99
  147.3 1.7 %copy.10 = f32[1,16,1,12,2,128]{5,4,3,2,1,0:T(2,128)} copy(f32[1,16,1,12,2,128]{5,3,4,1,2,0:T(8,128)} %bitcast.173) | data formatting | bytes 393216 | tf_op jit(solution)/shard_map/stack | solution.py:106
  (25 shorter events, 2.0 us)
Async XLA Ops:
  6.5 55.9 %all-gather.2.cloned.1.call-start = ((), (), s32[]{:S(2)}) async-start(), calls=%async_computation.1 | async-start | bytes 2359296 | tf_op jit(solution)/shard_map/all_gather | solution.py:86
  7.3 140.0 %reduce-scatter.2.cloned.1.call-start = ((), (), s32[]{:S(2)}) async-start(), calls=%async_computation.2 | async-start | bytes 2359296 | tf_op jit(solution)/shard_map/reduce_scatter | solution.py:99
  64.7 1.0 copy-start
Sparse Core Ops, SparseCore 0:
  9.4 53.0 all-gather.1
  80.7 66.5 reduce-scatter.1
where the time goes:
time: 156 us
  waiting for transfers between devices  117 us (75%)
  between operations  13.6 us (9%)
  matrix products  10.2 us (7%)
  local copies, waits for them, and re-layouts  9.68 us (6%)
  other arithmetic  5.64 us (4%)
    reduce_scatter x1, waiting for transfers between devices, on_device(): lax.psum_scatter(apply_gammas(jnp.stack(per_momentum, axis=1), gamma_mix,...  66.7 us
    all_gather x1, waiting for transfers between devices, on_device(): gathered = lax.all_gather(perambulator, 'space', axis=4, tiled=True)  49.2 us
    dot_general x1, matrix products, apply_gammas(): jnp.einsum('gostk,apstkb->apgob', gamma_mix, blocks, precision=lax.Precis...  3.8 us
  transfers between devices with their start and end apart: 2, of which 2 were waited for; matrix products, arithmetic and copies ran while one was open for 4% of the time, Pallas kernels for 0%

commit v1 on v0

--- a/solution.py
+++ b/solution.py
@@ -3,6 +3,7 @@
 import jax.numpy as jnp
 from jax import lax
 from jax.sharding import PartitionSpec as P
+from jax.lax import all_gather
 
 LY = 48
 LZ = 48
@@ -83,7 +84,8 @@
     site_ids = lax.axis_index("space") * local_sites + jnp.arange(local_sites, dtype=jnp.int32)
     cosine, sine = phase_tables(momenta, site_ids, extent_x)
     gamma_mix = gamma_mixer(gamma_columns, gamma_phases)
-    gathered = lax.all_gather(perambulator, "space", axis=4, tiled=True)
+    w2 = all_gather(perambulator, axis_name="space")
+    gathered = jnp.concatenate(w2, axis=4)
     chosen = jnp.take(gathered, source_slots, axis=1)
     vectors = eigvecs[0].reshape(local_sites * 3, 2 * eig_count)
     left_real, left_imag = sink_vectors(vectors, chosen[0, 0])

time: 156 us -> 156 us (level)
  no operation moved by 1% of the time
where the time goes in v1:
time: 156 us
  waiting for transfers between devices  117 us (75%)
  between operations  13.6 us (9%)
  matrix products  10.2 us (7%)
  local copies, waits for them, and re-layouts  9.68 us (6%)
  other arithmetic  5.64 us (4%)
    reduce_scatter x1, waiting for transfers between devices, on_device(): lax.psum_scatter(apply_gammas(jnp.stack(per_momentum, axis=1), gamma_mix,...  66.7 us
    all_gather x1, waiting for transfers between devices, on_device(): w2 = all_gather(perambulator, axis_name='space')  49.2 us
    dot_general x1, matrix products, apply_gammas(): jnp.einsum('gostk,apstkb->apgob', gamma_mix, blocks, precision=lax.Precis...  3.8 us
  transfers between devices with their start and end apart: 2, of which 2 were waited for; matrix products, arithmetic and copies ran while one was open for 4% of the time, Pallas kernels for 0%

profile of v1, /device:TPU:0, one launch (start us, length us, event | category | flops | bytes accessed | tf_op | source)
XLA Modules:
  0.0 155.9 jit_solution(15535519684010389070)
XLA Ops:
  6.5 0.7 all-gather.3.cloned.1.call-update
  7.3 1.3 fusion.137
  8.6 1.3 fusion.109
  10.5 0.7 compare_select_fusion
  11.2 0.7 convert_subtract_fusion
  11.9 0.7 fusion.124
  12.6 0.7 compare_and_fusion
  13.3 49.2 %all-gather.3.cloned.1.call-done = bf16[8,8,4,2,16,128]{5,4,0,3,2,1:T(8,128)(2,1)} async-done(((bf16[1,8,4,2,16,128]{5,4,0,3,2,1:T(8,128)(2,1)}), bf16[8,8,4,2,16,128]{5,4,0,3,2,1:T(8,128)(2,1)}) %all-gather.3.cloned.1.call-update) | async-done | bytes 2097168 | tf_op jit(solution)/shard_map/all_gather | solution.py:87
  62.5 2.2 %gather_fusion = bf16[2,4,2,128,128]{4,3,2,1,0:T(8,128)(2,1)S(1)} fusion(bf16[8,4,2,128,128]{4,3,2,1,0:T(8,128)(2,1)} %bitcast.180, s32[1024]{0:T(1024)S(1)} %pad_clamp_fusion), kind=kCustom, calls=%fused_computation | custom fusion | bytes 1048584 | tf_op jit(solution)/shard_map/jit(_take)/gather | solution.py:89
  65.0 0.7 copy-done
  66.4 0.3 fusion.9
  66.7 0.3 fusion.10
  67.0 0.3 fusion.11
  67.6 0.3 fusion.13
  68.0 0.3 fusion.14
  68.3 1.1 fusion.26
  69.3 1.1 fusion.25
  70.4 1.1 fusion.6
  71.5 1.1 fusion.5
  72.5 1.5 maximum_bitcast_fusion
  74.0 2.7 %copy.14 = f32[128,4,4,2,128,1]{4,2,1,3,5,0:T(4,128)S(1)} copy(f32[128,4,4,2,128,1]{0,4,1,2,3,5:T(8,128)} %maximum_bitcast_fusion) | data formatting | bytes 4194304 | tf_op jit(solution)/shard_map/stack | solution.py:100
  76.7 3.8 %fusion = f32[128,1,12,2,128]{4,2,3,0,1:T(8,128)} fusion(f32[128,4,4,2,128,1]{4,2,1,3,5,0:T(4,128)S(1)} %copy.14, f32[12,1,4,4,2]{0,3,2,4,1:T(4,128)S(1)} %get-tuple-element.48, f32[12,1,4,4,2]{0,3,2,4,1:T(4,128)S(1)} %get-tuple-element.47), kind=kOutput, calls=%fused_computation.7 | convolution fusion | flops 151388928 | bytes 3673088 | tf_op jit(solution)/shard_map/gostk,apstkb->apgob/dot_general | solution.py:25
  80.6 66.7 %reduce-scatter.2.cloned.1.call-done = f32[16,1,12,2,128]{4,2,3,0,1:T(8,128)} async-done(((f32[128,1,12,2,128]{4,2,3,0,1:T(8,128)}), f32[16,1,12,2,128]{4,2,3,0,1:T(8,128)}) %reduce-scatter.2.cloned.1.call-update) | async-done | bytes 196624 | tf_op jit(solution)/shard_map/reduce_scatter | solution.py:101
  147.3 1.7 %copy.11 = f32[1,16,1,12,2,128]{5,4,3,2,1,0:T(2,128)} copy(f32[1,16,1,12,2,128]{5,3,4,1,2,0:T(8,128)} %bitcast.178) | data formatting | bytes 393216 | tf_op jit(solution)/shard_map/stack | solution.py:108
  (25 shorter events, 2.0 us)
Async XLA Ops:
  6.5 55.9 %all-gather.3.cloned.1.call-start = ((), (), s32[]{:S(2)}) async-start(), calls=%async_computation.2 | async-start | bytes 2359296 | tf_op jit(solution)/shard_map/all_gather | solution.py:87
  7.3 140.0 %reduce-scatter.2.cloned.1.call-start = ((), (), s32[]{:S(2)}) async-start(), calls=%async_computation.1 | async-start | bytes 2359296 | tf_op jit(solution)/shard_map/reduce_scatter | solution.py:101
  64.7 1.0 copy-start
Sparse Core Ops, SparseCore 0:
  9.4 53.0 all-gather.2
  80.7 66.5 reduce-scatter.1
